TPU v7x, 32 devices: a whole 2x2x4 slice. The times are simulated.
32 devices in a mesh: pipe: 4 (over y, core), vocab: 2 (over x), expert: 4 (over z).
Axes of the slice: x: 2, y: 2, z: 4, core: 2. Of those that a mesh axis runs over, the one named last changes fastest.
Arguments:
- token_ids: int32 [192], replicated, may hold values from 0 to 65535
- routes: int32 [192, 2], replicated, may hold values from 0 to 3, all different within a row; in each aligned block of 192 rows (0 to 191, 192 to 383, ...) at most 144 rows name the same one
- gate_weights: float32 [192, 2], replicated, may hold values from 0.2 to 1
- embed_table: bfloat16 [65536, 7168], P(('pipe', 'vocab'), 'expert'), may hold values from -0.59765625 to 0.59765625
- w_gate: bfloat16 [4, 7168, 2048], P('expert', None, ('pipe', 'vocab')), may hold values from -0.5 to 0.5
- w_up: bfloat16 [4, 7168, 2048], P('expert', None, ('pipe', 'vocab')), may hold values from -0.5 to 0.5
- w_down: bfloat16 [4, 2048, 7168], P('expert', ('pipe', 'vocab')), may hold values from -0.125 to 0.125
Outputs:
- logits: bfloat16 [192, 65536], P('expert', ('pipe', 'vocab'))
Inputs may be any that keep to these rules, and one draw needn't show every extreme that they name: `routes`: each row names 2 different experts; over all 192 rows no expert is named more than 144 times, a bound that some block reaches.
All inputs are finite; a program needn't handle non-finite values.
Results may differ from a plain program's by a relative error of at most 0.025.
Values may be sent and summed in bfloat16 or wider, within the bound.
A program may use at most 128 MiB of HBM per device.

v0:
```python
import jax
import jax.numpy as jnp
from jax import lax
from jax.sharding import PartitionSpec as P


def per_device(token_ids, routes, gate_weights, embed_table, w_gate, w_up, w_down):
    vocab_rows, width_cols = embed_table.shape
    tokens, top_count = routes.shape
    experts = lax.axis_size("expert")
    group_size = lax.axis_size(("pipe", "vocab"))
    capacity = group_size * (3 * tokens * top_count // (2 * experts * group_size))
    row_base = lax.axis_index(("pipe", "vocab")) * vocab_rows
    local_ids = token_ids - row_base
    in_shard = (local_ids >= 0) & (local_ids < vocab_rows)
    lookup_rows = jnp.take(embed_table, jnp.clip(local_ids, 0, vocab_rows - 1), axis=0)
    lookup_rows = jnp.where(in_shard[:, None], lookup_rows.astype(jnp.float32), 0.0)
    embedded = lax.psum(lookup_rows.astype(jnp.bfloat16), ("pipe", "vocab"))
    flat_routes = routes.reshape(-1)
    one_hot = (flat_routes[:, None] == jnp.arange(experts, dtype=jnp.int32)[None, :]).astype(
        jnp.int32
    )
    slot_index = jnp.sum((jnp.cumsum(one_hot, axis=0) - one_hot) * one_hot, axis=1)
    slot_dest = flat_routes * capacity + slot_index
    repeated = jnp.repeat(embedded, top_count, axis=0)
    buffer = jnp.zeros((experts * capacity, width_cols), jnp.bfloat16).at[slot_dest].set(repeated)
    buffer = buffer.reshape(experts, capacity, width_cols)
    flat_rows = lax.all_to_all(buffer, "expert", split_axis=0, concat_axis=2, tiled=True)[0]
    gate_proj = jnp.dot(flat_rows, w_gate[0], preferred_element_type=jnp.float32)
    up_proj = jnp.dot(flat_rows, w_up[0], preferred_element_type=jnp.float32)
    hidden = (jax.nn.silu(gate_proj) * up_proj).astype(jnp.bfloat16)
    partial_value = jnp.dot(hidden, w_down[0], preferred_element_type=jnp.float32)[None]
    shared = lax.psum_scatter(
        partial_value.astype(jnp.bfloat16), ("pipe", "vocab"), scatter_dimension=1, tiled=True
    ).astype(jnp.float32)
    shared = lax.all_to_all(
        shared.astype(jnp.bfloat16), "expert", split_axis=2, concat_axis=0, tiled=True
    ).astype(shared.dtype)
    returned = lax.all_gather(
        shared.astype(jnp.bfloat16), ("pipe", "vocab"), axis=1, tiled=True
    ).astype(shared.dtype)
    picked = returned.reshape(experts * capacity, width_cols)[slot_dest].reshape(
        tokens, top_count, width_cols
    )
    moe_out = jnp.sum(picked * gate_weights[:, :, None], axis=1)
    residual = (embedded.astype(jnp.float32) + moe_out).astype(jnp.bfloat16)
    return lax.psum_scatter(
        lax.dot_general(
            residual, embed_table, (((1,), (1,)), ((), ())), preferred_element_type=jnp.float32
        ).astype(jnp.bfloat16),
        "expert",
        scatter_dimension=0,
        tiled=True,
    )


def solution(mesh):
    return jax.shard_map(
        per_device,
        mesh=mesh,
        in_specs=(
            P(),
            P(),
            P(),
            P(("pipe", "vocab"), "expert"),
            P("expert", None, ("pipe", "vocab")),
            P("expert", None, ("pipe", "vocab")),
            P("expert", ("pipe", "vocab"), None),
        ),
        out_specs=P("expert", ("pipe", "vocab")),
        check_vma=False,
    )
```

profile of v0, /device:TPU:0, one launch (start us, length us, event | category | flops | bytes accessed | tf_op | source)
XLA Modules:
  0.0 428.2 jit_solution(8567750402209135640)
XLA Ops:
  6.5 0.7 compare_and_fusion
  7.2 14.9 %gather_fusion = bf16[192,1792]{1,0:T(8,128)(2,1)S(1)} fusion(bf16[8192,1792]{1,0:T(8,128)(2,1)} %param.10, s32[1024]{0:T(1024)S(1)} %pad_clamp_fusion.1), kind=kCustom, calls=%fused_computation | custom fusion | bytes 1377024 | tf_op jit(solution)/shard_map/jit(_take)/gather | solution.py:16
  22.1 1.2 select_convert_fusion
  23.8 1.2 reduce-window.6
  25.9 55.8 %all-reduce.4.cloned.1.call-done = bf16[192,1792]{1,0:T(8,128)(2,1)} async-done(((bf16[192,1792]{1,0:T(8,128)(2,1)}), bf16[192,1792]{1,0:T(8,128)(2,1)}) %all-reduce.4.cloned.1.call-update) | async-done | bytes 688144 | tf_op jit(solution)/shard_map/psum | solution.py:18
  81.6 1.8 broadcast_in_dim.42
  84.0 3.3 scatter_custom_fusion
  87.3 51.2 %all_to_all.33 = bf16[4,144,1792]{2,1,0:T(8,128)(2,1)S(1)} all-to-all(bf16[4,144,1792]{2,1,0:T(8,128)(2,1)S(1)} %bitcast.66), channel_id=1, replica_groups=mesh['pipe'=4,'vocab'=2,'expert'=4] {'expert'}, dimensions={0} | all-to-all | bytes 4128768 | tf_op jit(solution)/shard_map/all_to_all | solution.py:28
  138.5 1.1 copy.41
  139.8 1.8 copy-done
  141.6 0.8 fusion.5
  142.4 6.9 %fusion.1 = bf16[1,144,7168]{2,1,0:T(8,128)(2,1)} fusion(bf16[1,256,7168]{2,1,0:T(8,128)(2,1)} %param.13, bf16[144,7168]{1,0:T(8,128)(2,1)S(1)} %bitcast.63, bf16[1,7168,256]{2,1,0:T(8,128)(2,1)} %param.12, f32[144,256]{1,0:T(8,128)S(1)} %fusion.5), kind=kOutput, calls=%fused_computation.5 | convolution fusion | flops 1058217984 | bytes 11616256 | tf_op jit(solution)/shard_map/dot_general | solution.py:32
  149.2 58.3 %fusion = bf16[24,7168]{1,0:T(8,128)(2,1)S(1)} fusion(bf16[1,144,7168]{2,1,0:T(8,128)(2,1)} %fusion.1), kind=kCustom, calls=%all-reduce-scatter | all-reduce-scatter fusion | flops 1376257 | bytes 2408960
  207.6 1.9 collective-permute-start
  209.6 1.7 collective-permute-start.1
  212.6 4.5 %collective-permute-done = bf16[24,7168]{1,0:T(8,128)(2,1)S(1)} collective-permute-done((bf16[24,7168]{1,0:T(8,128)(2,1)S(1)}, bf16[24,7168]{1,0:T(8,128)(2,1)S(1)}, u32[]{:S(2)}, u32[]{:S(2)}) %collective-permute-start) | collective-permute-done | bytes 344096
  217.0 4.8 %concatenate = bf16[66,7168]{1,0:T(8,128)(2,1)S(1)} concatenate(bf16[18,7168]{1,0:T(8,128)(2,1)S(1)} %collective-permute-done.1, bf16[24,7168]{1,0:T(8,128)(2,1)S(1)} %collective-permute-done, bf16[24,7168]{1,0:T(8,128)(2,1)S(1)} %fusion), dimensions={0} | concatenate | bytes 1892352
  222.0 6.0 %copy.42 = bf16[1,18,7168]{1,0,2:T(2,128)(2,1)} copy(bf16[1,18,7168]{2,1,0:T(8,128)(2,1)S(1)} %dynamic-slice_bitcast_fusion) | data formatting | bytes 516096 | tf_op jit(solution)/shard_map/reduce_scatter | solution.py:33
  228.5 39.8 %reduce.4 = bf16[7168,18]{1,0:T(8,128)(2,1)S(1)} reduce(bf16[7168,1,18]{2,1,0:T(2,128)(2,1)} %bitcast.64, bf16[]{:T(256)} %broadcast.68), dimensions={1}, to_apply=%bitcast.56.reduce_sub_computation | reduce | bytes 516098
  268.3 3.4 reshape.114
  271.7 9.8 %all_to_all.34 = bf16[4,2,16128]{2,1,0:T(2,128)(2,1)S(1)} all-to-all(bf16[4,2,16128]{2,1,0:T(2,128)(2,1)S(1)} %reshape.114), channel_id=1, replica_groups=mesh['pipe'=4,'vocab'=2,'expert'=4] {'expert'}, dimensions={0} | all-to-all | bytes 516096 | tf_op jit(solution)/shard_map/all_to_all | solution.py:36
  281.4 5.2 %reshape.115 = bf16[7168,1,18]{2,1,0:T(2,128)(2,1)} reshape(bf16[4,2,16128]{2,1,0:T(2,128)(2,1)S(1)} %all_to_all.34) | data formatting | bytes 516096
  286.6 7.3 %copy.43 = bf16[1,18,7168]{2,1,0:T(8,128)(2,1)S(1)} copy(bf16[1,18,7168]{1,0,2:T(2,128)(2,1)} %bitcast.65) | data formatting | bytes 516096 | tf_op jit(solution)/shard_map/all_to_all | solution.py:36
  293.9 0.8 all_to_all.28
  295.1 29.7 %all-gather.3.cloned.1.call-done = bf16[4,1,144,1792]{3,0,1,2:T(4,128)(2,1)} async-done(((bf16[4,1,18,1792]{3,0,1,2:T(4,128)(2,1)}), bf16[4,1,144,1792]{3,0,1,2:T(4,128)(2,1)}) %all-gather.3.cloned.1.call-update) | async-done | bytes 2064400 | tf_op jit(solution)/shard_map/all_gather | solution.py:39
  324.8 1.8 copy.45
  326.6 2.4 bitcast_convert_fusion
  329.0 6.1 %gather_fusion.1 = f32[384,1792]{1,0:T(8,128)S(1)} fusion(f32[576,1792]{1,0:T(8,128)} %bitcast_convert_fusion, s32[1024]{0:T(1024)S(1)} %pad_clamp_fusion), kind=kCustom, calls=%fused_computation.1 | custom fusion | bytes 5506560 | tf_op jit(solution)/shard_map/gather | solution.py:42
  335.1 2.8 reshape.75
  337.8 5.9 %multiply_reduce_fusion = f32[192,1792]{1,0:T(8,128)S(1)} fusion(f32[192,2,1792]{2,1,0:T(2,128)} %reshape.75, f32[192,2]{1,0:T(8,128)S(1)} %copy.46), kind=kLoop, calls=%fused_computation.11 | loop fusion | flops 1032192 | bytes 4130304 | tf_op jit(solution)/shard_map/reduce_sum | solution.py:45
  343.8 17.4 %convolution_convert_fusion = bf16[192,8192]{1,0:T(8,128)(2,1)} fusion(bf16[8192,1792]{1,0:T(8,128)(2,1)} %param.10, f32[192,1792]{1,0:T(8,128)S(1)} %multiply_reduce_fusion, bf16[192,1792]{1,0:T(8,128)(2,1)S(1)} %copy-done.1), kind=kOutput, calls=%fused_computation.3 | convolution fusion | flops 5639749632 | bytes 34570240 | tf_op jit(solution)/shard_map/dot_general | solution.py:48
  361.1 60.6 %reduce-scatter.5.cloned.1.call-done = bf16[48,8192]{1,0:T(8,128)(2,1)} async-done(((bf16[192,8192]{1,0:T(8,128)(2,1)}), bf16[48,8192]{1,0:T(8,128)(2,1)}) %reduce-scatter.5.cloned.1.call-update) | async-done | bytes 786448 | tf_op jit(solution)/shard_map/reduce_scatter | solution.py:47
  (37 shorter events, 3.8 us)
Async XLA Ops:
  6.5 75.1 %all-reduce.4.cloned.1.call-start = ((), (), s32[]{:S(2)}) async-start(), calls=%async_computation.3 | async-start | bytes 1376256 | tf_op jit(solution)/shard_map/psum | solution.py:18
  22.1 1.3 copy-start.2
  23.3 301.5 %all-gather.3.cloned.1.call-start = ((), (), s32[]{:S(2)}) async-start(), calls=%async_computation.5 | async-start | bytes 2322432 | tf_op jit(solution)/shard_map/all_gather | solution.py:39
  139.5 2.0 copy-start
  149.2 62.1 %copy-start.4 = (u32[32]{0:T(128)S(1)}, u32[32]{0:T(128)}, u32[]{:S(2)}) copy-start(u32[32]{0:T(128)} %constant.54) | copy-start | bytes 388
  207.6 9.5 %collective-permute-start = (bf16[24,7168]{1,0:T(8,128)(2,1)S(1)}, bf16[24,7168]{1,0:T(8,128)(2,1)S(1)}, u32[]{:S(2)}, u32[]{:S(2)}) collective-permute-start(bf16[24,7168]{1,0:T(8,128)(2,1)S(1)} %fusion), channel_id=1, source_target_pairs={{0,4},{4,8},{8,12},{12,16},{16,20},{20,24},{24,28},{1,5},{5,9},{9,... | collective-permute-start | bytes 1032200
  209.6 3.0 collective-permute-start.1
  286.6 8.4 %copy-start.3 = (f32[192,2]{0,1:T(2,128)S(1)}, f32[192,2]{0,1:T(2,128)}, u32[]{:S(2)}) copy-start(f32[192,2]{0,1:T(2,128)} %param.9) | copy-start | bytes 4612
  294.7 127.0 %reduce-scatter.5.cloned.1.call-start = ((), (), s32[]{:S(2)}) async-start(), calls=%async_computation.4 | async-start | bytes 3932160 | tf_op jit(solution)/shard_map/reduce_scatter | solution.py:47
  337.8 5.9 %copy-start.1 = (bf16[192,1792]{1,0:T(8,128)(2,1)S(1)}, bf16[192,1792]{1,0:T(8,128)(2,1)}, u32[]{:S(2)}) copy-start(bf16[192,1792]{1,0:T(8,128)(2,1)} %all-reduce.4.cloned.1.call-done) | copy-start | bytes 2064388
Sparse Core Ops, SparseCore 0:
  23.5 58.1 all-reduce.3
  294.8 29.9 all-gather.2
  361.3 60.3 reduce-scatter.4
where the time goes:
time: 429 us; the launch traced here: 428 us
  waiting for transfers between devices  151 us (35%)
  blocking collectives  119 us (28%)
  local copies, waits for them, and re-layouts  64 us (15%)
  other arithmetic  51.5 us (12%)
  matrix products  25 us (6%)
  between operations  14 us (3%)
    reduce_scatter x1, waiting for transfers between devices, per_device(): lax.psum_scatter(lax.dot_general(residual, embed_table, (((1,), (1,)), ((...  60.6 us
    unnamed x1, blocking collectives  58.3 us
    psum x1, waiting for transfers between devices, per_device(): embedded = lax.psum(lookup_rows.astype(jnp.bfloat16), ('pipe', 'vocab'))  55.8 us
    all_to_all x1, blocking collectives, per_device(): lax.all_to_all(buffer, 'expert', split_axis=0, concat_axis=2, tiled=True)[0]  51.2 us
    unnamed x2, other arithmetic  39.8 us
    all_gather x1, waiting for transfers between devices, per_device(): lax.all_gather(shared.astype(jnp.bfloat16), ('pipe', 'vocab'), axis=1, ti...  29.7 us
    dot_general x1, matrix products, per_device(): lax.dot_general(residual, embed_table, (((1,), (1,)), ((), ())), preferre...  17.4 us
    unnamed x20, local copies, waits for them, and re-layouts  16.9 us
  transfers between devices with their start and end apart: 5, of which 4 were waited for; matrix products, arithmetic and copies ran while one was open for 1% of the time, Pallas kernels for 0%

commit v1 on v0

--- a/solution.py
+++ b/solution.py
@@ -2,6 +2,12 @@
 import jax.numpy as jnp
 from jax import lax
 from jax.sharding import PartitionSpec as P
+
+
+def gather_blocks(shard, name, along):
+    parts = lax.all_gather(shard, name, axis=0, tiled=False)
+    whole = jnp.concatenate(parts, axis=along)
+    return whole
 
 
 def per_device(token_ids, routes, gate_weights, embed_table, w_gate, w_up, w_down):
@@ -36,9 +42,7 @@
     shared = lax.all_to_all(
         shared.astype(jnp.bfloat16), "expert", split_axis=2, concat_axis=0, tiled=True
     ).astype(shared.dtype)
-    returned = lax.all_gather(
-        shared.astype(jnp.bfloat16), ("pipe", "vocab"), axis=1, tiled=True
-    ).astype(shared.dtype)
+    returned = gather_blocks(shared.astype(jnp.bfloat16), ("pipe", "vocab"), 1).astype(shared.dtype)
     picked = returned.reshape(experts * capacity, width_cols)[slot_dest].reshape(
         tokens, top_count, width_cols
     )

time: 429 us -> 458 us (1.068); the launches traced: 428 us -> 450 us
  local copies, waits for them, and re-layouts: 64 us -> 79.9 us
    convert_element_type x0 -> x3, local copies, waits for them, and re-layouts: none -> 17.5 us  [per_device(): gather_blocks(shared.astype(jnp.bfloat16), ('pipe', 'vocab'), 1)]
where the time goes in v1:
time: 458 us; the launch traced here: 450 us
  waiting for transfers between devices  153 us (33%)
  blocking collectives  120 us (26%)
  local copies, waits for them, and re-layouts  79.9 us (17%)
  other arithmetic  53.3 us (12%)
  matrix products  25.2 us (6%)
  between operations  14.3 us (3%)
    reduce_scatter x1, waiting for transfers between devices, per_device(): lax.psum_scatter(lax.dot_general(residual, embed_table, (((1,), (1,)), ((...  60.6 us
    unnamed x1, blocking collectives  58.3 us
    psum x1, waiting for transfers between devices, per_device(): embedded = lax.psum(lookup_rows.astype(jnp.bfloat16), ('pipe', 'vocab'))  55.8 us
    all_to_all x1, blocking collectives, per_device(): lax.all_to_all(buffer, 'expert', split_axis=0, concat_axis=2, tiled=True)[0]  51.6 us
    unnamed x2, other arithmetic  39.8 us
    all_gather x1, waiting for transfers between devices, gather_blocks(): parts = lax.all_gather(shard, name, axis=0, tiled=False)  32.6 us
    dot_general x1, matrix products, per_device(): lax.dot_general(residual, embed_table, (((1,), (1,)), ((), ())), preferre...  17.6 us
    convert_element_type x3, local copies, waits for them, and re-layouts, per_device(): gather_blocks(shared.astype(jnp.bfloat16), ('pipe', 'vocab'), 1)  17.5 us
  transfers between devices with their start and end apart: 5, of which 4 were waited for; matrix products, arithmetic and copies ran while one was open for 1% of the time, Pallas kernels for 0%

profile of v1, /device:TPU:0, one launch (start us, length us, event | category | flops | bytes accessed | tf_op | source)
XLA Modules:
  0.0 449.7 jit_solution(6012752432301147784)
XLA Ops:
  7.2 14.9 %gather_fusion = bf16[192,1792]{1,0:T(8,128)(2,1)S(1)} fusion(bf16[8192,1792]{1,0:T(8,128)(2,1)} %param.10, s32[1024]{0:T(1024)S(1)} %pad_clamp_fusion.1), kind=kCustom, calls=%fused_computation | custom fusion | bytes 1377024 | tf_op jit(solution)/shard_map/jit(_take)/gather | solution.py:22
  22.1 1.2 select_convert_fusion
  23.8 1.2 reduce-window.6
  25.9 55.8 %all-reduce.4.cloned.1.call-done = bf16[192,1792]{1,0:T(8,128)(2,1)} async-done(((bf16[192,1792]{1,0:T(8,128)(2,1)}), bf16[192,1792]{1,0:T(8,128)(2,1)}) %all-reduce.4.cloned.1.call-update) | async-done | bytes 688144 | tf_op jit(solution)/shard_map/psum | solution.py:24
  81.6 1.8 broadcast_in_dim.42
  84.0 3.3 scatter_custom_fusion
  87.3 51.6 %all_to_all.30 = bf16[4,144,1792]{2,1,0:T(8,128)(2,1)S(1)} all-to-all(bf16[4,144,1792]{2,1,0:T(8,128)(2,1)S(1)} %bitcast.67), channel_id=1, replica_groups=mesh['pipe'=4,'vocab'=2,'expert'=4] {'expert'}, dimensions={0} | all-to-all | bytes 4128768 | tf_op jit(solution)/shard_map/all_to_all | solution.py:34
  138.9 1.1 copy.42
  140.3 1.8 copy-done
  142.1 0.8 fusion.5
  142.8 6.9 %fusion.1 = bf16[1,144,7168]{2,1,0:T(8,128)(2,1)} fusion(bf16[1,256,7168]{2,1,0:T(8,128)(2,1)} %param.13, bf16[144,7168]{1,0:T(8,128)(2,1)S(1)} %bitcast.63, bf16[1,7168,256]{2,1,0:T(8,128)(2,1)} %param.12, f32[144,256]{1,0:T(8,128)S(1)} %fusion.5), kind=kOutput, calls=%fused_computation.5 | convolution fusion | flops 1058217984 | bytes 11616256 | tf_op jit(solution)/shard_map/dot_general | solution.py:38
  149.7 58.3 %fusion = bf16[24,7168]{1,0:T(8,128)(2,1)S(1)} fusion(bf16[1,144,7168]{2,1,0:T(8,128)(2,1)} %fusion.1), kind=kCustom, calls=%all-reduce-scatter | all-reduce-scatter fusion | flops 1376257 | bytes 2408960
  208.0 2.0 collective-permute-start
  210.1 1.7 collective-permute-start.1
  213.0 4.5 collective-permute-done
  217.5 4.8 %concatenate = bf16[66,7168]{1,0:T(8,128)(2,1)S(1)} concatenate(bf16[18,7168]{1,0:T(8,128)(2,1)S(1)} %collective-permute-done.1, bf16[24,7168]{1,0:T(8,128)(2,1)S(1)} %collective-permute-done, bf16[24,7168]{1,0:T(8,128)(2,1)S(1)} %fusion), dimensions={0} | concatenate | bytes 1892352
  222.4 6.0 %copy.43 = bf16[1,18,7168]{1,0,2:T(2,128)(2,1)} copy(bf16[1,18,7168]{2,1,0:T(8,128)(2,1)S(1)} %dynamic-slice_bitcast_fusion) | data formatting | bytes 516096 | tf_op jit(solution)/shard_map/reduce_scatter | solution.py:39
  229.0 39.8 %reduce.4 = bf16[7168,18]{1,0:T(8,128)(2,1)S(1)} reduce(bf16[7168,1,18]{2,1,0:T(2,128)(2,1)} %bitcast.65, bf16[]{:T(256)} %broadcast.68), dimensions={1}, to_apply=%bitcast.56.reduce_sub_computation | reduce | bytes 516098
  268.8 3.4 reshape.110
  272.1 9.7 %all_to_all.31 = bf16[4,2,16128]{2,1,0:T(2,128)(2,1)S(1)} all-to-all(bf16[4,2,16128]{2,1,0:T(2,128)(2,1)S(1)} %reshape.110), channel_id=1, replica_groups=mesh['pipe'=4,'vocab'=2,'expert'=4] {'expert'}, dimensions={0} | all-to-all | bytes 516096 | tf_op jit(solution)/shard_map/all_to_all | solution.py:42
  281.9 5.2 %reshape.111 = bf16[7168,1,18]{2,1,0:T(2,128)(2,1)} reshape(bf16[4,2,16128]{2,1,0:T(2,128)(2,1)S(1)} %all_to_all.31) | data formatting | bytes 516096
  287.1 7.3 %copy.44 = bf16[1,18,7168]{2,1,0:T(8,128)(2,1)S(1)} copy(bf16[1,18,7168]{1,0,2:T(2,128)(2,1)} %bitcast.66) | data formatting | bytes 516096 | tf_op jit(solution)/shard_map/all_to_all | solution.py:42
  295.6 32.6 %all-gather.3.cloned.1.call-done = bf16[32,1,18,1792]{3,2,1,0:T(8,128)(2,1)} async-done(((bf16[4,1,18,1792]{3,2,1,0:T(8,128)(2,1)}), bf16[32,1,18,1792]{3,2,1,0:T(8,128)(2,1)}) %all-gather.3.cloned.1.call-update) | async-done | bytes 2064400 | tf_op jit(solution)/shard_map/all_gather | solution.py:8
  328.3 4.2 copy_convert_fusion
  332.4 5.3 %reshape.101 = f32[8,4,18,1792]{3,1,0,2:T(4,128)} reshape(f32[32,1,18,1792]{3,0,2,1:T(8,128)} %copy_convert_fusion) | data formatting | bytes 8257536 | tf_op jit(solution)/shard_map/convert_element_type | solution.py:45
  337.8 7.0 %copy.47 = f32[4,8,18,1792]{3,2,1,0:T(8,128)} copy(f32[4,8,18,1792]{3,0,1,2:T(4,128)} %bitcast.64) | data formatting | bytes 8257536 | tf_op jit(solution)/shard_map/convert_element_type | solution.py:45
  344.8 5.2 %reshape.75 = f32[576,1792]{1,0:T(8,128)} reshape(f32[4,8,18,1792]{3,2,1,0:T(8,128)} %copy.47) | data formatting | bytes 8257536 | tf_op jit(solution)/shard_map/convert_element_type | solution.py:45
  350.0 6.1 %gather_fusion.1 = f32[384,1792]{1,0:T(8,128)S(1)} fusion(f32[576,1792]{1,0:T(8,128)} %reshape.75, s32[1024]{0:T(1024)S(1)} %pad_clamp_fusion), kind=kCustom, calls=%fused_computation.1 | custom fusion | bytes 5506560 | tf_op jit(solution)/shard_map/gather | solution.py:46
  356.1 2.8 reshape.74
  358.9 5.9 %multiply_reduce_fusion = f32[192,1792]{1,0:T(8,128)S(1)} fusion(f32[192,2,1792]{2,1,0:T(2,128)} %reshape.74, f32[192,2]{1,0:T(8,128)S(1)} %copy.48), kind=kLoop, calls=%fused_computation.11 | loop fusion | flops 1032192 | bytes 4130304 | tf_op jit(solution)/shard_map/reduce_sum | solution.py:49
  364.8 17.6 %convolution_convert_fusion = bf16[192,8192]{1,0:T(8,128)(2,1)} fusion(bf16[8192,1792]{1,0:T(8,128)(2,1)} %param.10, f32[192,1792]{1,0:T(8,128)S(1)} %multiply_reduce_fusion, bf16[192,1792]{1,0:T(8,128)(2,1)S(1)} %copy-done.1), kind=kOutput, calls=%fused_computation.3 | convolution fusion | flops 5639749632 | bytes 34570240 | tf_op jit(solution)/shard_map/dot_general | solution.py:52
  382.4 60.6 %reduce-scatter.5.cloned.1.call-done = bf16[48,8192]{1,0:T(8,128)(2,1)} async-done(((bf16[192,8192]{1,0:T(8,128)(2,1)}), bf16[48,8192]{1,0:T(8,128)(2,1)}) %reduce-scatter.5.cloned.1.call-update) | async-done | bytes 786448 | tf_op jit(solution)/shard_map/reduce_scatter | solution.py:51
  (40 shorter events, 5.3 us)
Async XLA Ops:
  6.5 75.1 %all-reduce.4.cloned.1.call-start = ((), (), s32[]{:S(2)}) async-start(), calls=%async_computation.3 | async-start | bytes 1376256 | tf_op jit(solution)/shard_map/psum | solution.py:24
  7.2 16.2 %copy-start.2 = (s32[192,2]{0,1:T(2,128)S(1)}, s32[192,2]{0,1:T(2,128)}, u32[]{:S(2)}) copy-start(s32[192,2]{0,1:T(2,128)} %param.8) | copy-start | bytes 4612
  23.4 304.9 %all-gather.3.cloned.1.call-start = ((), (), s32[]{:S(2)}) async-start(), calls=%async_computation.5 | async-start | bytes 3096576 | tf_op jit(solution)/shard_map/all_gather | solution.py:8
  140.0 2.0 copy-start
  149.7 62.1 %copy-start.4 = (u32[32]{0:T(128)S(1)}, u32[32]{0:T(128)}, u32[]{:S(2)}) copy-start(u32[32]{0:T(128)} %constant.54) | copy-start | bytes 388
  208.0 9.5 %collective-permute-start = (bf16[24,7168]{1,0:T(8,128)(2,1)S(1)}, bf16[24,7168]{1,0:T(8,128)(2,1)S(1)}, u32[]{:S(2)}, u32[]{:S(2)}) collective-permute-start(bf16[24,7168]{1,0:T(8,128)(2,1)S(1)} %fusion), channel_id=1, source_target_pairs={{0,4},{4,8},{8,12},{12,16},{16,20},{20,24},{24,28},{1,5},{5,9},{9,... | collective-permute-start | bytes 1032200
  210.1 3.0 collective-permute-start.1
  287.1 8.4 %copy-start.3 = (f32[192,2]{0,1:T(2,128)S(1)}, f32[192,2]{0,1:T(2,128)}, u32[]{:S(2)}) copy-start(f32[192,2]{0,1:T(2,128)} %param.9) | copy-start | bytes 4612
  295.3 147.7 %reduce-scatter.5.cloned.1.call-start = ((), (), s32[]{:S(2)}) async-start(), calls=%async_computation.4 | async-start | bytes 3932160 | tf_op jit(solution)/shard_map/reduce_scatter | solution.py:51
  358.9 5.9 %copy-start.1 = (bf16[192,1792]{1,0:T(8,128)(2,1)S(1)}, bf16[192,1792]{1,0:T(8,128)(2,1)}, u32[]{:S(2)}) copy-start(bf16[192,1792]{1,0:T(8,128)(2,1)} %all-reduce.4.cloned.1.call-done) | copy-start | bytes 2064388
Sparse Core Ops, SparseCore 0:
  23.5 58.1 all-reduce.3
  295.4 32.8 all-gather.2
  382.5 60.3 reduce-scatter.4
